TPU v7x, 256 devices: a whole 4x4x8 slice. The times are simulated.
256 devices in a mesh: replica: 2 (over core), fsdp: 128 (over z, x, y).
Axes of the slice: x: 4, y: 4, z: 8, core: 2. Of those that a mesh axis runs over, the one named last changes fastest.
Arguments:
- activations: bfloat16 [131072, 4096], P(('replica', 'fsdp')), may hold values from -24 to 24
- queries: bfloat16 [131072, 2048], P(('replica', 'fsdp')), may hold values from -60 to 60
- out_grad: bfloat16 [131072, 2048], P(('replica', 'fsdp')), may hold values from -6 to 6
- lengths: int32 [512], P(('replica', 'fsdp')), may hold values from 32 to 256
- norm_gain: float32 [4096], replicated, may hold values from 0.5 to 7
- key_master: float32 [4096, 512], P('fsdp'), may hold values from -0.09375 to 0.09375
- value_master: float32 [4096, 512], P('fsdp'), may hold values from -0.09375 to 0.09375
Outputs:
- key_direction: float32 [4096, 512], P('fsdp')
- value_direction: float32 [4096, 512], P('fsdp')
All inputs are finite; a program needn't handle non-finite values.
Results may differ from a plain program's by a relative error of at most 0.009.
The roundings to bfloat16 on the way count: a program that leaves them out, or rounds other values in their place, can miss the bound.
Values may be sent and summed in bfloat16 or wider, within the bound.
No kernel may reach another device: no remote copies, remote signals or barrier semaphores. Data moves between devices by JAX's collectives and lax.ppermute only.
A program may use at most 128 MiB of HBM per device.

v0:
```python
import functools

import jax
import jax.numpy as jnp
from jax import lax
from jax.experimental import pallas as pl
from jax.experimental.pallas import tpu as pltpu
from jax.sharding import Mesh
from jax.sharding import PartitionSpec as P


D = 4096
HD = 128
GROUP = 4
LEN = 256
EPS = 1e-5
ZN, XN, YN = 8, 4, 4
FSDP = ("z", "x", "y")
ALL = ("r", "z", "x", "y")
BF = jnp.bfloat16
F32 = jnp.float32


def plane_pairs(phase, step):
    pairs = []
    for r in range(2):
        along_x = (r == 1) == (phase == 1)
        for z in range(ZN):
            for x in range(XN):
                for y in range(YN):
                    to = ((x + step) % XN, y) if along_x else (x, (y + step) % YN)
                    here = ((r * ZN + z) * XN + x) * YN + y
                    pairs.append((here, ((r * ZN + z) * XN + to[0]) * YN + to[1]))
    return pairs


def shift(a, phase, step):
    return lax.ppermute(a, ALL, plane_pairs(phase, step))


def to_partner(a):
    return lax.ppermute(a, "r", [(0, 1), (1, 0)])


def exchange(blocks, axes):
    return lax.all_to_all(blocks, axes, split_axis=0, concat_axis=0, tiled=True)


def in_hbm(a):
    return pltpu.with_memory_space_constraint(a, pltpu.HBM)


def cast_kernel(key, value, own, key_in, value_in, sems):
    cols = pl.ds(pl.multiple_of(lax.axis_index("r") * 2 * HD, 2 * HD), 2 * HD)
    loads = [
        pltpu.make_async_copy(key.at[:, cols], key_in, sems.at[0]),
        pltpu.make_async_copy(value.at[:, cols], value_in, sems.at[1]),
    ]
    for c in loads:
        c.start()
    for c in loads:
        c.wait()
    for h in range(2):
        own[h, :, :HD] = key_in[:, h * HD : (h + 1) * HD].astype(BF)
        own[h, :, HD:] = value_in[:, h * HD : (h + 1) * HD].astype(BF)


def cast(key, value):
    rows = key.shape[0]
    hbm = pl.BlockSpec(memory_space=pltpu.HBM)
    return pl.pallas_call(
        cast_kernel,
        in_specs=[hbm, hbm],
        out_specs=pl.BlockSpec(memory_space=pltpu.VMEM),
        out_shape=pltpu.VMEM((2, rows, 2 * HD), BF),
        scratch_shapes=[
            pltpu.VMEM((rows, 2 * HD), F32),
            pltpu.VMEM((rows, 2 * HD), F32),
            pltpu.SemaphoreType.DMA((2,)),
        ],
        compiler_params=pltpu.CompilerParams(vmem_limit_bytes=4 * 2**20),
        name="cast",
    )(in_hbm(key), in_hbm(value))


ROWS = 64


def prep_kernel(where, act, queries, grad, gain, send, kept, rows_in, grad_in, gain_in, sems):
    tokens, half = act.shape[0], queries.shape[1] // 2
    steps = tokens // ROWS
    mine = pl.multiple_of(where[0] * half, half)
    other = pl.multiple_of((1 - where[0]) * half, half)
    swap = pltpu.make_async_copy(queries.at[:, pl.ds(other, half)], send.at[:, pl.ds(D, half)], sems.at[2 * steps])

    def loads(i):
        at = pl.ds(pl.multiple_of(i * ROWS, ROWS), ROWS)
        return (
            pltpu.make_async_copy(act.at[at], rows_in.at[at], sems.at[i]),
            pltpu.make_async_copy(grad.at[at], grad_in.at[at], sems.at[steps + i]),
        )

    for i in range(steps):
        for c in loads(i):
            c.start()
    swap.start()
    gain_load = pltpu.make_async_copy(gain, gain_in, sems.at[2 * steps + 1])
    gain_load.start()
    gain_load.wait()
    zero = jnp.zeros((ROWS, half), BF)

    def step(i, _):
        at = pl.ds(pl.multiple_of(i * ROWS, ROWS), ROWS)
        for c in loads(i):
            c.wait()
        a = rows_in[at].astype(F32)
        inverse = lax.rsqrt(jnp.mean(a * a, axis=-1, keepdims=True) + EPS)
        send[at, :D] = (a * inverse * gain_in[...]).astype(BF)
        seq = i // (LEN // ROWS)
        live = i * ROWS - seq * LEN + lax.broadcasted_iota(jnp.int32, (ROWS, 1), 0) < where[6 + seq]
        send[at, D + half :] = jnp.where(live, grad_in[at, pl.ds(other, half)], zero)
        kept[at] = jnp.where(live, grad_in[at, pl.ds(mine, half)], zero)
        return 0

    lax.fori_loop(0, steps, step, 0)
    swap.wait()


def prepare(where, act, queries, grad, gain):
    tokens, width = act.shape[0], queries.shape[1]
    vmem = pl.BlockSpec(memory_space=pltpu.VMEM)
    smem = pl.BlockSpec(memory_space=pltpu.SMEM)
    hbm = pl.BlockSpec(memory_space=pltpu.HBM)
    return pl.pallas_call(
        prep_kernel,
        in_specs=[smem, hbm, hbm, hbm, hbm],
        out_specs=[vmem, vmem],
        out_shape=[
            pltpu.VMEM((tokens, D + width), BF),
            pltpu.VMEM((tokens, width // 2), BF),
        ],
        scratch_shapes=[
            pltpu.VMEM((tokens, D), BF),
            pltpu.VMEM((tokens, width), BF),
            pltpu.VMEM((1, D), F32),
            pltpu.SemaphoreType.DMA((2 * (tokens // ROWS) + 2,)),
        ],
        compiler_params=pltpu.CompilerParams(vmem_limit_bytes=24 * 2**20),
        cost_estimate=pl.CostEstimate(flops=1_000_000_000, transcendentals=512, bytes_accessed=16_000_000),
        name="prep",
    )(where, *(in_hbm(a) for a in (act, queries, grad, gain.reshape(1, D))))


def sum_kernel(parts, full):
    full[...] = functools.reduce(jnp.add, [parts[i].astype(F32) for i in range(ZN)])


def gather_sum(parts):
    vmem = pl.BlockSpec(memory_space=pltpu.VMEM)
    return pl.pallas_call(
        sum_kernel,
        in_specs=[vmem],
        out_specs=vmem,
        out_shape=pltpu.VMEM(parts.shape[1:], F32),
        compiler_params=pltpu.CompilerParams(vmem_limit_bytes=4 * 2**20),
        name="gather_sum",
    )(parts)


def square_kernel(full, theirs, square):
    total = jnp.sum(full[...] * full[...]) + jnp.sum(theirs[...] * theirs[...])
    square[...] = jnp.full(square.shape, total, F32)


def squares(full, theirs):
    vmem = pl.BlockSpec(memory_space=pltpu.VMEM)
    return pl.pallas_call(
        square_kernel,
        in_specs=[vmem] * 2,
        out_specs=vmem,
        out_shape=pltpu.VMEM((128, 1, 128), F32),
        compiler_params=pltpu.CompilerParams(vmem_limit_bytes=4 * 2**20),
        name="squares",
    )(full, theirs)


def finish_kernel(where, squares, full, theirs, key, value):
    total = jnp.sum(squares[...]) / 128
    scale = jnp.sqrt(jnp.float32(2 * D * 512)) / jnp.sqrt(total + 1e-6)
    for r in range(2):
        for h in range(2):
            both = jnp.where(where[0] == r, full[h], theirs[h]) * scale
            cols = slice((2 * r + h) * HD, (2 * r + h + 1) * HD)
            key[:, cols] = both[:, :HD]
            value[:, cols] = both[:, HD:]


def finish(where, squares, full, theirs):
    vmem = pl.BlockSpec(memory_space=pltpu.VMEM)
    like = jax.ShapeDtypeStruct((32, 4 * HD), F32)
    return pl.pallas_call(
        finish_kernel,
        in_specs=[pl.BlockSpec(memory_space=pltpu.SMEM)] + [vmem] * 3,
        out_specs=[vmem] * 2,
        out_shape=[like, like],
        compiler_params=pltpu.CompilerParams(vmem_limit_bytes=4 * 2**20),
        name="finish",
    )(where, squares, full, theirs)


NT = (((1,), (1,)), ((), ()))


def head_kernel(which, where, w0, w1, w2, w3, sent, came, queries, kept, g0, g1, g2, g3, w, kv, dkvt, block):
    half = queries.shape[0]
    wide = GROUP * HD
    own = pl.multiple_of(which[0] * wide, wide)
    base = pl.multiple_of(where[0] * (queries.shape[1] // 2) + own, wide)
    qcol = D + own
    gcol = D + queries.shape[1] // 2 + own
    p1, p2, s1, s2 = where[1], where[2], where[3], where[4]

    def chunk_at(o1, o2):
        return pl.multiple_of((lax.rem(p1 + o1, 4) * s1 + lax.rem(p2 + o2, 4) * s2) * 32, 32)

    def level_at(i):
        return i * 512

    for o2, source in enumerate((w0, w1, w2, w3)):
        for o1 in range(4):
            at = chunk_at(o1, o2)
            for z in range(ZN):
                w[pl.ds(level_at(z) + at, 32)] = source[o1, z]

    def project(s):
        source = sent if s * LEN < half else came
        at = s * LEN % half
        kv[s * LEN : (s + 1) * LEN] = jnp.dot(source[at : at + LEN, :D], w[...], preferred_element_type=F32).astype(BF)

    project(0)
    scale = 1.0 / HD**0.5
    top = HD
    below = lax.broadcasted_iota(jnp.int32, (top, top), 0) <= lax.broadcasted_iota(jnp.int32, (top, top), 1)

    def stacked(ref, rows, col):
        return jnp.concatenate([ref[rows, pl.ds(col + g * HD, HD)] for g in range(GROUP)], axis=0)

    def soft(parts):
        peak = functools.reduce(jnp.maximum, [jnp.max(a, axis=0, keepdims=True) for a in parts])
        parts = [jnp.exp(a - peak) for a in parts]
        inverse = 1.0 / functools.reduce(jnp.add, [jnp.sum(a, axis=0, keepdims=True) for a in parts])
        return [a * inverse for a in parts]

    def strip(key, value, value_t, qs, gs):
        keys = key.shape[0]
        score = lax.dot_general(key, qs, NT, preferred_element_type=F32)
        dp = lax.dot_general(value, gs, NT, preferred_element_type=F32)
        ps, pbs = [], []
        for g in range(GROUP):
            cols = slice(g * top, (g + 1) * top)
            parts = [score[i : i + top, cols] * scale for i in range(0, keys, top)]
            parts[-1] = jnp.where(below, parts[-1], -1e30)
            p = jnp.concatenate(soft(parts), axis=0)
            ps.append(p)
            pbs.append(p.astype(BF))
        pb = jnp.concatenate(pbs, axis=1)
        out_t = jnp.dot(value_t, pb, preferred_element_type=F32).astype(BF).astype(F32)
        delta = jnp.sum(gs.T.astype(F32) * out_t, axis=0, keepdims=True)
        ds = []
        for g in range(GROUP):
            cols = slice(g * top, (g + 1) * top)
            ds.append((ps[g] * (dp[:, cols] - delta[:, cols])).astype(BF))
        ds = jnp.concatenate(ds, axis=1)
        return jnp.dot(ds, qs, preferred_element_type=F32), jnp.dot(pb, gs, preferred_element_type=F32)

    for s in range(2 * half // LEN):
        rows = slice(s * LEN, (s + 1) * LEN)
        at = s * LEN % half
        qref, qat, gref, gat = (queries, base, kept, own) if s * LEN < half else (came, qcol, came, gcol)
        key, value = kv[rows, :HD], kv[rows, HD:]
        value_t = value.T
        if (s + 1) * LEN < 2 * half:
            project(s + 1)
        early, late = slice(at, at + top), slice(at + top, at + LEN)
        dk0, dv0 = strip(key[:top], value[:top], value_t[:, :top], stacked(qref, early, qat), stacked(gref, early, gat))
        dk1, dv1 = strip(key, value, value_t, stacked(qref, late, qat), stacked(gref, late, gat))
        dk = jnp.concatenate([dk1[:top] + dk0, dk1[top:]], axis=0)
        dv = jnp.concatenate([dv1[:top] + dv0, dv1[top:]], axis=0)
        both = jnp.concatenate([(dk * scale).astype(BF), dv.astype(BF)], axis=1)
        dkvt[:, rows] = both.T

    for z in range(ZN):
        cols = pl.ds(level_at(z), 512)
        part = jnp.dot(dkvt[:, :half], sent[:, cols], preferred_element_type=F32)
        part += jnp.dot(dkvt[:, half:], came[:, cols], preferred_element_type=F32)
        block[...] = part.astype(BF).T
        for o2, target in enumerate((g0, g1, g2, g3)):
            for o1 in range(4):
                target[o1, z] = block[pl.ds(chunk_at(o1, o2), 32)]


def one_head(head, where, pieces, sent, came, queries, kept):
    tokens = 2 * queries.shape[0]
    vmem = pl.BlockSpec(memory_space=pltpu.VMEM)
    cols = 2 * HD
    return pl.pallas_call(
        head_kernel,
        in_specs=[pl.BlockSpec(memory_space=pltpu.SMEM)] * 2 + [vmem] * 8,
        out_specs=[vmem] * 4,
        out_shape=[jax.ShapeDtypeStruct((4, ZN, 32, cols), BF)] * 4,
        scratch_shapes=[
            pltpu.VMEM((D, cols), BF),
            pltpu.VMEM((tokens, cols), BF),
            pltpu.VMEM((cols, tokens), BF),
            pltpu.VMEM((512, cols), BF),
        ],
        compiler_params=pltpu.CompilerParams(vmem_limit_bytes=30 * 2**20),
        cost_estimate=pl.CostEstimate(flops=8_000_000_000, transcendentals=1_000_000, bytes_accessed=16_000_000),
        name="head",
    )(jnp.full((1,), head, jnp.int32), where, *pieces, sent, came, queries, kept)


def local(activations, queries, out_grad, lengths, norm_gain, key_master, value_master):
    r, z, x, y = (lax.axis_index(a) for a in ALL)
    first = r == 0
    where = jnp.stack([
        r,
        jnp.where(first, y, x), jnp.where(first, x, y),
        jnp.where(first, 1, 4), jnp.where(first, 4, 1),
        z, lengths[0], lengths[1],
    ]).astype(jnp.int32)

    own = cast(key_master, value_master)
    level = exchange(jnp.broadcast_to(own[None], (ZN, *own.shape)), "z")
    sent, kept = prepare(where, activations, queries, out_grad, norm_gain)
    came = to_partner(sent)
    gathered = [level]
    for o in (1, 2, 3):
        gathered.append(shift(level, 1, -o))
    pieces = []
    for head in range(2):
        block = jnp.stack([a[:, head] for a in gathered])
        pieces.append([block] + [shift(block, 2, -o) for o in (1, 2, 3)])
    parts = []
    for head in range(2):
        g = one_head(head, where, pieces[head], sent, came, queries, kept)
        got = [g[0]] + [shift(g[o], 2, o) for o in (1, 2, 3)]
        line = sum(a.astype(F32) for a in got).astype(BF)
        got = [line[0]] + [shift(line[o], 1, o) for o in (1, 2, 3)]
        parts.append(sum(a.astype(F32) for a in got).astype(BF))
    part = exchange(jnp.stack(parts, axis=1), "z")
    full = gather_sum(part)
    theirs = to_partner(full)
    square = squares(full, theirs)
    return finish(where, exchange(square, FSDP), full, theirs)


def solution(mesh):
    split = Mesh(mesh.devices.reshape(2, ZN, XN, YN), ALL)
    in_specs = (P(ALL, None), P(ALL, None), P(ALL, None), P(ALL), P(), P(FSDP, None), P(FSDP, None))
    out_specs = (P(FSDP, None), P(FSDP, None))


    return jax.shard_map(local, mesh=split, in_specs=in_specs, out_specs=out_specs, check_vma=False)
```

profile of v0, /device:TPU:32, one launch (start us, length us, event | category | flops | bytes accessed | tf_op | source)
XLA Modules:
  0.0 151.5 jit_solution(9060511321626872562)
XLA Ops:
  0.6 0.7 stack.42.where
  1.4 6.0 %prep.1 = (bf16[512,6144]{1,0:T(8,128)(2,1)S(1)}, bf16[512,1024]{1,0:T(8,128)(2,1)S(1)}) custom-call(s32[8]{0:T(128)S(1)} %stack.42.where, bf16[512,4096]{1,0:T(8,128)(2,1)} %act.1, bf16[512,2048]{1,0:T(8,128)(2,1)} %queries.5, bf16[512,2048]{1,0:T(8,128)(2,1)} %grad.1, f32[1,4096]{1,0:T(1,128)} %bitcast.49), custom_call_target="tpu_custom_call" | custom-call | flops 1000000000 | bytes 16000000 | tf_op jit(solution)/shard_map/prep/pallas_call | solution.py:134
  7.4 0.1 collective-permute-start.6
  7.5 0.9 cast.1
  8.5 19.3 %all_to_all.15 = bf16[8,2,32,256]{3,2,1,0:T(8,128)(2,1)S(1)} all-to-all(bf16[8,2,32,256]{3,2,1,0:T(8,128)(2,1)S(1)} %broadcast_in_dim.2), channel_id=1, replica_groups=mesh['r'=2,'z'=8,'x'=4,'y'=4] {'z'}, dimensions={0} | all-to-all | bytes 524288 | tf_op jit(solution)/shard_map/all_to_all | solution.py:46
  27.8 3.1 %collective-permute-start = (bf16[8,2,32,256]{3,2,0,1:T(8,128)(2,1)S(1)}, bf16[8,2,32,256]{3,2,0,1:T(8,128)(2,1)S(1)}, u32[]{:S(2)}, u32[]{:S(2)}) collective-permute-start(bf16[8,2,32,256]{3,2,0,1:T(8,128)(2,1)S(1)} %copy.9), channel_id=1, source_target_pairs={{0,3},{1,0},{2,1},{3,2},{4,7},{5,4},{6,5},{7,6},{8,11},{9,8},{10,9... | collective-permute-start | bytes 786440 | tf_op jit(solution)/shard_map/ppermute | solution.py:38
  30.9 0.6 collective-permute-start.1
  31.6 1.0 collective-permute-start.2
  32.5 5.1 %collective-permute-done = bf16[8,2,32,256]{3,2,0,1:T(8,128)(2,1)S(1)} collective-permute-done((bf16[8,2,32,256]{3,2,0,1:T(8,128)(2,1)S(1)}, bf16[8,2,32,256]{3,2,0,1:T(8,128)(2,1)S(1)}, u32[]{:S(2)}, u32[]{:S(2)}) %collective-permute-start) | collective-permute-done | bytes 262176 | tf_op jit(solution)/shard_map/ppermute | solution.py:38
  37.6 1.3 collective-permute-done.1
  38.9 2.7 %collective-permute-done.2 = bf16[8,2,32,256]{3,2,0,1:T(8,128)(2,1)S(1)} collective-permute-done((bf16[8,2,32,256]{3,2,0,1:T(8,128)(2,1)S(1)}, bf16[8,2,32,256]{3,2,0,1:T(8,128)(2,1)S(1)}, u32[]{:S(2)}, u32[]{:S(2)}) %collective-permute-start.2) | collective-permute-done | bytes 262176 | tf_op jit(solution)/shard_map/ppermute | solution.py:38
  41.6 0.1 pad_maximum_fusion.w0
  41.7 2.8 %collective-permute-start.3 = (bf16[4,8,32,256]{3,2,1,0:T(8,128)(2,1)S(1)}, bf16[4,8,32,256]{3,2,1,0:T(8,128)(2,1)S(1)}, u32[]{:S(2)}, u32[]{:S(2)}) collective-permute-start(bf16[4,8,32,256]{3,2,1,0:T(8,128)(2,1)S(1)} %pad_maximum_fusion.w0), channel_id=1, source_target_pairs={{0,12},{1,13},{2,14},{3,15},{4,0},{5,1},{6,2},{7,3},{8,4},{9,5},{1... | collective-permute-start | bytes 1572872 | tf_op jit(solution)/shard_map/ppermute | solution.py:38
  44.5 0.8 collective-permute-start.4
  45.3 0.9 collective-permute-start.5
  46.2 0.1 pad_maximum_fusion.1.w0
  46.3 2.4 %collective-permute-start.13 = (bf16[4,8,32,256]{3,2,1,0:T(8,128)(2,1)S(1)}, bf16[4,8,32,256]{3,2,1,0:T(8,128)(2,1)S(1)}, u32[]{:S(2)}, u32[]{:S(2)}) collective-permute-start(bf16[4,8,32,256]{3,2,1,0:T(8,128)(2,1)S(1)} %pad_maximum_fusion.1.w0), channel_id=1, source_target_pairs={{0,12},{1,13},{2,14},{3,15},{4,0},{5,1},{6,2},{7,3},{8,4},{9,5},{1... | collective-permute-start | bytes 1572872 | tf_op jit(solution)/shard_map/ppermute | solution.py:38
  48.7 8.2 %collective-permute-done.3.w1 = bf16[4,8,32,256]{3,2,1,0:T(8,128)(2,1)S(1)} collective-permute-done((bf16[4,8,32,256]{3,2,1,0:T(8,128)(2,1)S(1)}, bf16[4,8,32,256]{3,2,1,0:T(8,128)(2,1)S(1)}, u32[]{:S(2)}, u32[]{:S(2)}) %collective-permute-start.3) | collective-permute-done | bytes 524320 | tf_op jit(solution)/shard_map/ppermute | solution.py:38
  56.9 4.5 %collective-permute-start.15 = (bf16[4,8,32,256]{3,2,1,0:T(8,128)(2,1)S(1)}, bf16[4,8,32,256]{3,2,1,0:T(8,128)(2,1)S(1)}, u32[]{:S(2)}, u32[]{:S(2)}) collective-permute-start(bf16[4,8,32,256]{3,2,1,0:T(8,128)(2,1)S(1)} %pad_maximum_fusion.1.w0), channel_id=1, source_target_pairs={{0,4},{1,5},{2,6},{3,7},{4,8},{5,9},{6,10},{7,11},{8,12},{9,13},{1... | collective-permute-start | bytes 1572872 | tf_op jit(solution)/shard_map/ppermute | solution.py:38
  61.4 9.7 %head.2 = (bf16[4,8,32,256]{3,2,1,0:T(8,128)(2,1)S(1)}, bf16[4,8,32,256]{3,2,1,0:T(8,128)(2,1)S(1)}, bf16[4,8,32,256]{3,2,1,0:T(8,128)(2,1)S(1)}, bf16[4,8,32,256]{3,2,1,0:T(8,128)(2,1)S(1)}) custom-call(s32[1]{0:T(128)} %constant.26.clone.1.which, s32[8]{0:T(128)S(1)} %stack.42.where, bf16[4,8,32,256]{3,2,1,0:T(8,128)(2,1)S(1)} %pad_maximum_fusion.w0, ...), custom_call_target="tpu_custom_call" | custom-call | flops 8000000000 | bytes 16000000 | tf_op jit(solution)/shard_map/head/pallas_call | solution.py:306
  71.1 0.1 collective-permute-start.7
  71.2 1.5 collective-permute-start.8
  72.6 1.8 %collective-permute-start.9 = (bf16[4,8,32,256]{3,2,1,0:T(8,128)(2,1)S(1)}, bf16[4,8,32,256]{3,2,1,0:T(8,128)(2,1)S(1)}, u32[]{:S(2)}, u32[]{:S(2)}) collective-permute-start(bf16[4,8,32,256]{3,2,1,0:T(8,128)(2,1)S(1)} %get-tuple-element.17), channel_id=1, source_target_pairs={{0,12},{1,13},{2,14},{3,15},{4,0},{5,1},{6,2},{7,3},{8,4},{9,5},{1... | collective-permute-start | bytes 1572872 | tf_op jit(solution)/shard_map/ppermute | solution.py:38
  74.4 9.6 %head.3 = (bf16[4,8,32,256]{3,2,1,0:T(8,128)(2,1)S(1)}, bf16[4,8,32,256]{3,2,1,0:T(8,128)(2,1)S(1)}, bf16[4,8,32,256]{3,2,1,0:T(8,128)(2,1)S(1)}, bf16[4,8,32,256]{3,2,1,0:T(8,128)(2,1)S(1)}) custom-call(s32[1]{0:T(128)} %constant.27.clone.1.which, s32[8]{0:T(128)S(1)} %stack.42.where, bf16[4,8,32,256]{3,2,1,0:T(8,128)(2,1)S(1)} %pad_maximum_fusion.1.w0, ...), custom_call_target="tpu_custom_call" | custom-call | flops 8000000000 | bytes 16000000 | tf_op jit(solution)/shard_map/head/pallas_call | solution.py:306
  84.1 0.9 collective-permute-start.16
  85.0 2.2 %collective-permute-start.17 = (bf16[4,8,32,256]{3,2,1,0:T(8,128)(2,1)S(1)}, bf16[4,8,32,256]{3,2,1,0:T(8,128)(2,1)S(1)}, u32[]{:S(2)}, u32[]{:S(2)}) collective-permute-start(bf16[4,8,32,256]{3,2,1,0:T(8,128)(2,1)S(1)} %get-tuple-element.20), channel_id=1, source_target_pairs={{0,8},{1,9},{2,10},{3,11},{4,12},{5,13},{6,14},{7,15},{8,0},{9,1},... | collective-permute-start | bytes 1572872 | tf_op jit(solution)/shard_map/ppermute | solution.py:38
  87.2 2.5 %collective-permute-start.18 = (bf16[4,8,32,256]{3,2,1,0:T(8,128)(2,1)S(1)}, bf16[4,8,32,256]{3,2,1,0:T(8,128)(2,1)S(1)}, u32[]{:S(2)}, u32[]{:S(2)}) collective-permute-start(bf16[4,8,32,256]{3,2,1,0:T(8,128)(2,1)S(1)} %get-tuple-element.21), channel_id=1, source_target_pairs={{0,12},{1,13},{2,14},{3,15},{4,0},{5,1},{6,2},{7,3},{8,4},{9,5},{1... | collective-permute-start | bytes 1572872 | tf_op jit(solution)/shard_map/ppermute | solution.py:38
  89.7 0.4 add_convert_fusion.1
  90.1 0.1 collective-permute-start.10
  90.2 2.1 %collective-permute-start.11 = (bf16[8,32,256]{2,1,0:T(8,128)(2,1)S(1)}, bf16[8,32,256]{2,1,0:T(8,128)(2,1)S(1)}, u32[]{:S(2)}, u32[]{:S(2)}) collective-permute-start(bf16[8,32,256]{2,1,0:T(8,128)(2,1)S(1)} %get-tuple-element.24), channel_id=1, source_target_pairs={{0,2},{1,3},{2,0},{3,1},{4,6},{5,7},{6,4},{7,5},{8,10},{9,11},{10,... | collective-permute-start | bytes 393224 | tf_op jit(solution)/shard_map/ppermute | solution.py:38
  92.3 8.0 %collective-permute-done.16 = bf16[4,8,32,256]{3,2,1,0:T(8,128)(2,1)S(1)} collective-permute-done((bf16[4,8,32,256]{3,2,1,0:T(8,128)(2,1)S(1)}, bf16[4,8,32,256]{3,2,1,0:T(8,128)(2,1)S(1)}, u32[]{:S(2)}, u32[]{:S(2)}) %collective-permute-start.16) | collective-permute-done | bytes 524320 | tf_op jit(solution)/shard_map/ppermute | solution.py:38
  100.3 2.6 %collective-permute-start.12 = (bf16[8,32,256]{2,1,0:T(8,128)(2,1)S(1)}, bf16[8,32,256]{2,1,0:T(8,128)(2,1)S(1)}, u32[]{:S(2)}, u32[]{:S(2)}) collective-permute-start(bf16[8,32,256]{2,1,0:T(8,128)(2,1)S(1)} %get-tuple-element.23), channel_id=1, source_target_pairs={{0,3},{1,0},{2,1},{3,2},{4,7},{5,4},{6,5},{7,6},{8,11},{9,8},{10,9... | collective-permute-start | bytes 393224 | tf_op jit(solution)/shard_map/ppermute | solution.py:38
  103.0 0.4 collective-permute-done.17
  103.4 1.9 %collective-permute-done.18 = bf16[4,8,32,256]{3,2,1,0:T(8,128)(2,1)S(1)} collective-permute-done((bf16[4,8,32,256]{3,2,1,0:T(8,128)(2,1)S(1)}, bf16[4,8,32,256]{3,2,1,0:T(8,128)(2,1)S(1)}, u32[]{:S(2)}, u32[]{:S(2)}) %collective-permute-start.18) | collective-permute-done | bytes 524320 | tf_op jit(solution)/shard_map/ppermute | solution.py:38
  105.3 0.4 add_convert_fusion
  105.7 0.1 collective-permute-start.19
  105.8 2.0 %collective-permute-start.20 = (bf16[8,32,256]{2,1,0:T(8,128)(2,1)S(1)}, bf16[8,32,256]{2,1,0:T(8,128)(2,1)S(1)}, u32[]{:S(2)}, u32[]{:S(2)}) collective-permute-start(bf16[8,32,256]{2,1,0:T(8,128)(2,1)S(1)} %get-tuple-element.27), channel_id=1, source_target_pairs={{0,2},{1,3},{2,0},{3,1},{4,6},{5,7},{6,4},{7,5},{8,10},{9,11},{10,... | collective-permute-start | bytes 393224 | tf_op jit(solution)/shard_map/ppermute | solution.py:38
  107.8 1.2 collective-permute-start.21
  109.0 0.1 fusion.6
  109.1 4.3 %collective-permute-done.19 = bf16[8,32,256]{2,1,0:T(8,128)(2,1)S(1)} collective-permute-done((bf16[8,32,256]{2,1,0:T(8,128)(2,1)S(1)}, bf16[8,32,256]{2,1,0:T(8,128)(2,1)S(1)}, u32[]{:S(2)}, u32[]{:S(2)}) %collective-permute-start.19) | collective-permute-done | bytes 131104 | tf_op jit(solution)/shard_map/ppermute | solution.py:38
  113.3 0.9 collective-permute-done.21
  114.2 0.1 fusion.7
  114.4 13.3 %all_to_all.16.parts = bf16[8,2,32,256]{3,2,1,0:T(8,128)(2,1)S(1)} all-to-all(bf16[8,2,32,256]{3,2,1,0:T(8,128)(2,1)S(1)} %pad_maximum_fusion.2), channel_id=1, replica_groups=mesh['r'=2,'z'=8,'x'=4,'y'=4] {'z'}, dimensions={0} | all-to-all | bytes 524288 | tf_op jit(solution)/shard_map/all_to_all | solution.py:46
  127.7 0.1 collective-permute-start.22
  127.8 1.2 collective-permute-done.22.theirs
  129.0 0.2 squares.1
  129.2 20.8 %all_to_all.17.squares = f32[128,1,128]{2,1,0:T(1,128)S(1)} all-to-all(f32[128,1,128]{2,1,0:T(1,128)S(1)} %squares.1), channel_id=1, replica_groups=mesh['r'=2,'z'=8,'x'=4,'y'=4] {'z','x','y'}, dimensions={0} | all-to-all | bytes 131072 | tf_op jit(solution)/shard_map/all_to_all | solution.py:46
  150.0 1.5 %finish.1 = (f32[32,512]{1,0:T(8,128)}, f32[32,512]{1,0:T(8,128)}) custom-call(s32[8]{0:T(128)S(1)} %stack.42.where, f32[128,1,128]{2,1,0:T(1,128)S(1)} %all_to_all.17.squares, f32[2,32,256]{2,1,0:T(8,128)S(1)} %gather_sum.1.full, f32[2,32,256]{2,1,0:T(8,128)S(1)} %collective-permute-done.22.theirs), custom_call_target="tpu_custom_call" | custom-call | tf_op jit(solution)/shard_map/finish/pallas_call | solution.py:201
  (26 shorter events, 0.3 us)
Async XLA Ops:
  7.4 54.0 %copy-start = (bf16[512,2048]{1,0:T(8,128)(2,1)S(1)}, bf16[512,2048]{1,0:T(8,128)(2,1)}, u32[]{:S(2)}) copy-start(bf16[512,2048]{1,0:T(8,128)(2,1)} %queries.5) | copy-start | bytes 6291460
  7.4 54.0 %collective-permute-start.6 = (bf16[512,6144]{1,0:T(8,128)(2,1)S(1)}, bf16[512,6144]{1,0:T(8,128)(2,1)S(1)}, u32[]{:S(2)}, u32[]{:S(2)}) collective-permute-start(bf16[512,6144]{1,0:T(8,128)(2,1)S(1)} %get-tuple-element.12.sent), channel_id=1, source_target_pairs={{0,128},{128,0},{1,129},{129,1},{2,130},{130,2},{3,131},{131,3},{4... | collective-permute-start | bytes 18874376 | tf_op jit(solution)/shard_map/ppermute | solution.py:42
  27.8 9.8 %collective-permute-start = (bf16[8,2,32,256]{3,2,0,1:T(8,128)(2,1)S(1)}, bf16[8,2,32,256]{3,2,0,1:T(8,128)(2,1)S(1)}, u32[]{:S(2)}, u32[]{:S(2)}) collective-permute-start(bf16[8,2,32,256]{3,2,0,1:T(8,128)(2,1)S(1)} %copy.9), channel_id=1, source_target_pairs={{0,3},{1,0},{2,1},{3,2},{4,7},{5,4},{6,5},{7,6},{8,11},{9,8},{10,9... | collective-permute-start | bytes 786440 | tf_op jit(solution)/shard_map/ppermute | solution.py:38
  30.9 8.0 %collective-permute-start.1 = (bf16[8,2,32,256]{3,2,0,1:T(8,128)(2,1)S(1)}, bf16[8,2,32,256]{3,2,0,1:T(8,128)(2,1)S(1)}, u32[]{:S(2)}, u32[]{:S(2)}) collective-permute-start(bf16[8,2,32,256]{3,2,0,1:T(8,128)(2,1)S(1)} %copy.9), channel_id=1, source_target_pairs={{0,2},{1,3},{2,0},{3,1},{4,6},{5,7},{6,4},{7,5},{8,10},{9,11},{10,... | collective-permute-start | bytes 786440 | tf_op jit(solution)/shard_map/ppermute | solution.py:38
  31.6 10.1 %collective-permute-start.2 = (bf16[8,2,32,256]{3,2,0,1:T(8,128)(2,1)S(1)}, bf16[8,2,32,256]{3,2,0,1:T(8,128)(2,1)S(1)}, u32[]{:S(2)}, u32[]{:S(2)}) collective-permute-start(bf16[8,2,32,256]{3,2,0,1:T(8,128)(2,1)S(1)} %copy.9), channel_id=1, source_target_pairs={{0,1},{1,2},{2,3},{3,0},{4,5},{5,6},{6,7},{7,4},{8,9},{9,10},{10,1... | collective-permute-start | bytes 786440 | tf_op jit(solution)/shard_map/ppermute | solution.py:38
  41.7 15.2 %collective-permute-start.3 = (bf16[4,8,32,256]{3,2,1,0:T(8,128)(2,1)S(1)}, bf16[4,8,32,256]{3,2,1,0:T(8,128)(2,1)S(1)}, u32[]{:S(2)}, u32[]{:S(2)}) collective-permute-start(bf16[4,8,32,256]{3,2,1,0:T(8,128)(2,1)S(1)} %pad_maximum_fusion.w0), channel_id=1, source_target_pairs={{0,12},{1,13},{2,14},{3,15},{4,0},{5,1},{6,2},{7,3},{8,4},{9,5},{1... | collective-permute-start | bytes 1572872 | tf_op jit(solution)/shard_map/ppermute | solution.py:38
  44.5 12.4 %collective-permute-start.4 = (bf16[4,8,32,256]{3,2,1,0:T(8,128)(2,1)S(1)}, bf16[4,8,32,256]{3,2,1,0:T(8,128)(2,1)S(1)}, u32[]{:S(2)}, u32[]{:S(2)}) collective-permute-start(bf16[4,8,32,256]{3,2,1,0:T(8,128)(2,1)S(1)} %pad_maximum_fusion.w0), channel_id=1, source_target_pairs={{0,8},{1,9},{2,10},{3,11},{4,12},{5,13},{6,14},{7,15},{8,0},{9,1},... | collective-permute-start | bytes 1572872 | tf_op jit(solution)/shard_map/ppermute | solution.py:38
  45.3 16.1 %collective-permute-start.5 = (bf16[4,8,32,256]{3,2,1,0:T(8,128)(2,1)S(1)}, bf16[4,8,32,256]{3,2,1,0:T(8,128)(2,1)S(1)}, u32[]{:S(2)}, u32[]{:S(2)}) collective-permute-start(bf16[4,8,32,256]{3,2,1,0:T(8,128)(2,1)S(1)} %pad_maximum_fusion.w0), channel_id=1, source_target_pairs={{0,4},{1,5},{2,6},{3,7},{4,8},{5,9},{6,10},{7,11},{8,12},{9,13},{1... | collective-permute-start | bytes 1572872 | tf_op jit(solution)/shard_map/ppermute | solution.py:38
  46.3 26.3 %collective-permute-start.13 = (bf16[4,8,32,256]{3,2,1,0:T(8,128)(2,1)S(1)}, bf16[4,8,32,256]{3,2,1,0:T(8,128)(2,1)S(1)}, u32[]{:S(2)}, u32[]{:S(2)}) collective-permute-start(bf16[4,8,32,256]{3,2,1,0:T(8,128)(2,1)S(1)} %pad_maximum_fusion.1.w0), channel_id=1, source_target_pairs={{0,12},{1,13},{2,14},{3,15},{4,0},{5,1},{6,2},{7,3},{8,4},{9,5},{1... | collective-permute-start | bytes 1572872 | tf_op jit(solution)/shard_map/ppermute | solution.py:38
  56.9 17.5 %collective-permute-start.14 = (bf16[4,8,32,256]{3,2,1,0:T(8,128)(2,1)S(1)}, bf16[4,8,32,256]{3,2,1,0:T(8,128)(2,1)S(1)}, u32[]{:S(2)}, u32[]{:S(2)}) collective-permute-start(bf16[4,8,32,256]{3,2,1,0:T(8,128)(2,1)S(1)} %pad_maximum_fusion.1.w0), channel_id=1, source_target_pairs={{0,8},{1,9},{2,10},{3,11},{4,12},{5,13},{6,14},{7,15},{8,0},{9,1},... | collective-permute-start | bytes 1572872 | tf_op jit(solution)/shard_map/ppermute | solution.py:38
  56.9 17.5 %collective-permute-start.15 = (bf16[4,8,32,256]{3,2,1,0:T(8,128)(2,1)S(1)}, bf16[4,8,32,256]{3,2,1,0:T(8,128)(2,1)S(1)}, u32[]{:S(2)}, u32[]{:S(2)}) collective-permute-start(bf16[4,8,32,256]{3,2,1,0:T(8,128)(2,1)S(1)} %pad_maximum_fusion.1.w0), channel_id=1, source_target_pairs={{0,4},{1,5},{2,6},{3,7},{4,8},{5,9},{6,10},{7,11},{8,12},{9,13},{1... | collective-permute-start | bytes 1572872 | tf_op jit(solution)/shard_map/ppermute | solution.py:38
  71.1 16.1 %collective-permute-start.7 = (bf16[4,8,32,256]{3,2,1,0:T(8,128)(2,1)S(1)}, bf16[4,8,32,256]{3,2,1,0:T(8,128)(2,1)S(1)}, u32[]{:S(2)}, u32[]{:S(2)}) collective-permute-start(bf16[4,8,32,256]{3,2,1,0:T(8,128)(2,1)S(1)} %get-tuple-element.15), channel_id=1, source_target_pairs={{0,4},{1,5},{2,6},{3,7},{4,8},{5,9},{6,10},{7,11},{8,12},{9,13},{1... | collective-permute-start | bytes 1572872 | tf_op jit(solution)/shard_map/ppermute | solution.py:38
  71.2 18.5 %collective-permute-start.8 = (bf16[4,8,32,256]{3,2,1,0:T(8,128)(2,1)S(1)}, bf16[4,8,32,256]{3,2,1,0:T(8,128)(2,1)S(1)}, u32[]{:S(2)}, u32[]{:S(2)}) collective-permute-start(bf16[4,8,32,256]{3,2,1,0:T(8,128)(2,1)S(1)} %get-tuple-element.16), channel_id=1, source_target_pairs={{0,8},{1,9},{2,10},{3,11},{4,12},{5,13},{6,14},{7,15},{8,0},{9,1},... | collective-permute-start | bytes 1572872 | tf_op jit(solution)/shard_map/ppermute | solution.py:38
  72.6 17.1 %collective-permute-start.9 = (bf16[4,8,32,256]{3,2,1,0:T(8,128)(2,1)S(1)}, bf16[4,8,32,256]{3,2,1,0:T(8,128)(2,1)S(1)}, u32[]{:S(2)}, u32[]{:S(2)}) collective-permute-start(bf16[4,8,32,256]{3,2,1,0:T(8,128)(2,1)S(1)} %get-tuple-element.17), channel_id=1, source_target_pairs={{0,12},{1,13},{2,14},{3,15},{4,0},{5,1},{6,2},{7,3},{8,4},{9,5},{1... | collective-permute-start | bytes 1572872 | tf_op jit(solution)/shard_map/ppermute | solution.py:38
  84.1 16.3 %collective-permute-start.16 = (bf16[4,8,32,256]{3,2,1,0:T(8,128)(2,1)S(1)}, bf16[4,8,32,256]{3,2,1,0:T(8,128)(2,1)S(1)}, u32[]{:S(2)}, u32[]{:S(2)}) collective-permute-start(bf16[4,8,32,256]{3,2,1,0:T(8,128)(2,1)S(1)} %get-tuple-element.19), channel_id=1, source_target_pairs={{0,4},{1,5},{2,6},{3,7},{4,8},{5,9},{6,10},{7,11},{8,12},{9,13},{1... | collective-permute-start | bytes 1572872 | tf_op jit(solution)/shard_map/ppermute | solution.py:38
  85.0 18.4 %collective-permute-start.17 = (bf16[4,8,32,256]{3,2,1,0:T(8,128)(2,1)S(1)}, bf16[4,8,32,256]{3,2,1,0:T(8,128)(2,1)S(1)}, u32[]{:S(2)}, u32[]{:S(2)}) collective-permute-start(bf16[4,8,32,256]{3,2,1,0:T(8,128)(2,1)S(1)} %get-tuple-element.20), channel_id=1, source_target_pairs={{0,8},{1,9},{2,10},{3,11},{4,12},{5,13},{6,14},{7,15},{8,0},{9,1},... | collective-permute-start | bytes 1572872 | tf_op jit(solution)/shard_map/ppermute | solution.py:38
  87.2 18.1 %collective-permute-start.18 = (bf16[4,8,32,256]{3,2,1,0:T(8,128)(2,1)S(1)}, bf16[4,8,32,256]{3,2,1,0:T(8,128)(2,1)S(1)}, u32[]{:S(2)}, u32[]{:S(2)}) collective-permute-start(bf16[4,8,32,256]{3,2,1,0:T(8,128)(2,1)S(1)} %get-tuple-element.21), channel_id=1, source_target_pairs={{0,12},{1,13},{2,14},{3,15},{4,0},{5,1},{6,2},{7,3},{8,4},{9,5},{1... | collective-permute-start | bytes 1572872 | tf_op jit(solution)/shard_map/ppermute | solution.py:38
  90.1 17.6 %collective-permute-start.10 = (bf16[8,32,256]{2,1,0:T(8,128)(2,1)S(1)}, bf16[8,32,256]{2,1,0:T(8,128)(2,1)S(1)}, u32[]{:S(2)}, u32[]{:S(2)}) collective-permute-start(bf16[8,32,256]{2,1,0:T(8,128)(2,1)S(1)} %get-tuple-element.22), channel_id=1, source_target_pairs={{0,1},{1,2},{2,3},{3,0},{4,5},{5,6},{6,7},{7,4},{8,9},{9,10},{10,1... | collective-permute-start | bytes 393224 | tf_op jit(solution)/shard_map/ppermute | solution.py:38
  90.2 18.8 %collective-permute-start.11 = (bf16[8,32,256]{2,1,0:T(8,128)(2,1)S(1)}, bf16[8,32,256]{2,1,0:T(8,128)(2,1)S(1)}, u32[]{:S(2)}, u32[]{:S(2)}) collective-permute-start(bf16[8,32,256]{2,1,0:T(8,128)(2,1)S(1)} %get-tuple-element.24), channel_id=1, source_target_pairs={{0,2},{1,3},{2,0},{3,1},{4,6},{5,7},{6,4},{7,5},{8,10},{9,11},{10,... | collective-permute-start | bytes 393224 | tf_op jit(solution)/shard_map/ppermute | solution.py:38
  100.3 8.7 %collective-permute-start.12 = (bf16[8,32,256]{2,1,0:T(8,128)(2,1)S(1)}, bf16[8,32,256]{2,1,0:T(8,128)(2,1)S(1)}, u32[]{:S(2)}, u32[]{:S(2)}) collective-permute-start(bf16[8,32,256]{2,1,0:T(8,128)(2,1)S(1)} %get-tuple-element.23), channel_id=1, source_target_pairs={{0,3},{1,0},{2,1},{3,2},{4,7},{5,4},{6,5},{7,6},{8,11},{9,8},{10,9... | collective-permute-start | bytes 393224 | tf_op jit(solution)/shard_map/ppermute | solution.py:38
  105.7 7.7 %collective-permute-start.19 = (bf16[8,32,256]{2,1,0:T(8,128)(2,1)S(1)}, bf16[8,32,256]{2,1,0:T(8,128)(2,1)S(1)}, u32[]{:S(2)}, u32[]{:S(2)}) collective-permute-start(bf16[8,32,256]{2,1,0:T(8,128)(2,1)S(1)} %get-tuple-element.25), channel_id=1, source_target_pairs={{0,1},{1,2},{2,3},{3,0},{4,5},{5,6},{6,7},{7,4},{8,9},{9,10},{10,1... | collective-permute-start | bytes 393224 | tf_op jit(solution)/shard_map/ppermute | solution.py:38
  105.8 7.6 %collective-permute-start.20 = (bf16[8,32,256]{2,1,0:T(8,128)(2,1)S(1)}, bf16[8,32,256]{2,1,0:T(8,128)(2,1)S(1)}, u32[]{:S(2)}, u32[]{:S(2)}) collective-permute-start(bf16[8,32,256]{2,1,0:T(8,128)(2,1)S(1)} %get-tuple-element.27), channel_id=1, source_target_pairs={{0,2},{1,3},{2,0},{3,1},{4,6},{5,7},{6,4},{7,5},{8,10},{9,11},{10,... | collective-permute-start | bytes 393224 | tf_op jit(solution)/shard_map/ppermute | solution.py:38
  107.8 6.5 %collective-permute-start.21 = (bf16[8,32,256]{2,1,0:T(8,128)(2,1)S(1)}, bf16[8,32,256]{2,1,0:T(8,128)(2,1)S(1)}, u32[]{:S(2)}, u32[]{:S(2)}) collective-permute-start(bf16[8,32,256]{2,1,0:T(8,128)(2,1)S(1)} %get-tuple-element.26), channel_id=1, source_target_pairs={{0,3},{1,0},{2,1},{3,2},{4,7},{5,4},{6,5},{7,6},{8,11},{9,8},{10,9... | collective-permute-start | bytes 393224 | tf_op jit(solution)/shard_map/ppermute | solution.py:38
  127.7 1.3 collective-permute-start.22
where the time goes:
time: 153 us; the launch traced here: 151 us
  blocking collectives  53.3 us (35%)
  waiting for transfers between devices  34 us (22%)
  starting transfers between devices  33.4 us (22%)
  Pallas kernels  28 us (18%)
    all_to_all x3, blocking collectives, exchange(): return lax.all_to_all(blocks, axes, split_axis=0, concat_axis=0, tiled=True)  53.3 us
    ppermute x21, starting transfers between devices, shift(): return lax.ppermute(a, ALL, plane_pairs(phase, step))  33.2 us
    ppermute x21, waiting for transfers between devices, shift(): return lax.ppermute(a, ALL, plane_pairs(phase, step))  32.7 us
    pallas_call x2, Pallas kernels, one_head(): pl.pallas_call(head_kernel, in_specs=[pl.BlockSpec(memory_space=pltpu.SME...  19.3 us
    pallas_call x1, Pallas kernels, prepare(): pl.pallas_call(prep_kernel, in_specs=[smem, hbm, hbm, hbm, hbm], out_spec...  6.03 us
  transfers between devices with their start and end apart: 23, of which 10 were waited for; matrix products, arithmetic and copies ran while one was open for 1% of the time, Pallas kernels for 13%

commit v1 on v0

--- a/solution.py
+++ b/solution.py
@@ -100,12 +100,12 @@
             pltpu.make_async_copy(grad.at[at], grad_in.at[at], sems.at[steps + i]),
         )
 
+    gain_load = pltpu.make_async_copy(gain, gain_in, sems.at[2 * steps + 1])
+    gain_load.start()
     for i in range(steps):
         for c in loads(i):
             c.start()
     swap.start()
-    gain_load = pltpu.make_async_copy(gain, gain_in, sems.at[2 * steps + 1])
-    gain_load.start()
     gain_load.wait()
     zero = jnp.zeros((ROWS, half), BF)
 
@@ -340,11 +340,12 @@
     pieces = []
     for head in range(2):
         block = jnp.stack([a[:, head] for a in gathered])
-        pieces.append([block] + [shift(block, 2, -o) for o in (1, 2, 3)])
+        far = shift(block, 2, -2)
+        pieces.append([block, shift(block, 2, -1), far, shift(block, 2, -3)])
     parts = []
     for head in range(2):
         g = one_head(head, where, pieces[head], sent, came, queries, kept)
-        got = [g[0]] + [shift(g[o], 2, o) for o in (1, 2, 3)]
+        got = [g[0]] + [shift(g[o], 2, o) for o in (2, 1, 3)]
         line = sum(a.astype(F32) for a in got).astype(BF)
         got = [line[0]] + [shift(line[o], 1, o) for o in (1, 2, 3)]
         parts.append(sum(a.astype(F32) for a in got).astype(BF))

time: 153 us -> 148 us (0.967)
  starting transfers between devices: 33.4 us -> 31.3 us
  Pallas kernels: 28 us -> 26.2 us
  blocking collectives: 53.3 us -> 51.6 us
    ppermute x21, starting transfers between devices: 33.2 us -> 31.2 us  [shift(): return lax.ppermute(a, ALL, plane_pairs(phase, step))]
    pallas_call x1, Pallas kernels: 6.03 us -> 4.21 us  [prepare(): pl.pallas_call(prep_kernel, in_specs=[smem, hbm, hbm, hbm, hbm], out_spec...]
    all_to_all x3, blocking collectives: 53.3 us -> 51.6 us  [exchange(): return lax.all_to_all(blocks, axes, split_axis=0, concat_axis=0, tiled=True)]
  transfers between devices with their start and end apart: 23 -> 23, of which waited for: 10 -> 10; matrix products, arithmetic and copies ran while one was open for 1% -> 1% of each run, Pallas kernels for 13% -> 14%
where the time goes in v1:
time: 148 us; the launch traced here: 147 us
  blocking collectives  51.6 us (35%)
  waiting for transfers between devices  35.2 us (24%)
  starting transfers between devices  31.3 us (21%)
  Pallas kernels  26.2 us (18%)
    all_to_all x3, blocking collectives, exchange(): return lax.all_to_all(blocks, axes, split_axis=0, concat_axis=0, tiled=True)  51.6 us
    ppermute x21, waiting for transfers between devices, shift(): return lax.ppermute(a, ALL, plane_pairs(phase, step))  33.9 us
    ppermute x21, starting transfers between devices, shift(): return lax.ppermute(a, ALL, plane_pairs(phase, step))  31.2 us
    pallas_call x2, Pallas kernels, one_head(): pl.pallas_call(head_kernel, in_specs=[pl.BlockSpec(memory_space=pltpu.SME...  19.3 us
    pallas_call x1, Pallas kernels, prepare(): pl.pallas_call(prep_kernel, in_specs=[smem, hbm, hbm, hbm, hbm], out_spec...  4.21 us
  transfers between devices with their start and end apart: 23, of which 10 were waited for; matrix products, arithmetic and copies ran while one was open for 1% of the time, Pallas kernels for 14%

profile of v1, /device:TPU:32, one launch (start us, length us, event | category | flops | bytes accessed | tf_op | source)
XLA Modules:
  0.0 147.2 jit_solution(3986856426153944903)
XLA Ops:
  0.6 0.7 stack.42.where
  1.4 4.2 %prep.1 = (bf16[512,6144]{1,0:T(8,128)(2,1)S(1)}, bf16[512,1024]{1,0:T(8,128)(2,1)S(1)}) custom-call(s32[8]{0:T(128)S(1)} %stack.42.where, bf16[512,4096]{1,0:T(8,128)(2,1)} %act.1, bf16[512,2048]{1,0:T(8,128)(2,1)} %queries.5, bf16[512,2048]{1,0:T(8,128)(2,1)} %grad.1, f32[1,4096]{1,0:T(1,128)} %bitcast.49), custom_call_target="tpu_custom_call" | custom-call | flops 1000000000 | bytes 16000000 | tf_op jit(solution)/shard_map/prep/pallas_call | solution.py:134
  5.6 0.1 collective-permute-start.6
  5.7 0.9 cast.1
  6.7 19.3 %all_to_all.15 = bf16[8,2,32,256]{3,2,1,0:T(8,128)(2,1)S(1)} all-to-all(bf16[8,2,32,256]{3,2,1,0:T(8,128)(2,1)S(1)} %broadcast_in_dim.2), channel_id=1, replica_groups=mesh['r'=2,'z'=8,'x'=4,'y'=4] {'z'}, dimensions={0} | all-to-all | bytes 524288 | tf_op jit(solution)/shard_map/all_to_all | solution.py:46
  26.0 3.1 %collective-permute-start = (bf16[8,2,32,256]{3,2,0,1:T(8,128)(2,1)S(1)}, bf16[8,2,32,256]{3,2,0,1:T(8,128)(2,1)S(1)}, u32[]{:S(2)}, u32[]{:S(2)}) collective-permute-start(bf16[8,2,32,256]{3,2,0,1:T(8,128)(2,1)S(1)} %copy.9), channel_id=1, source_target_pairs={{0,3},{1,0},{2,1},{3,2},{4,7},{5,4},{6,5},{7,6},{8,11},{9,8},{10,9... | collective-permute-start | bytes 786440 | tf_op jit(solution)/shard_map/ppermute | solution.py:38
  29.1 0.6 collective-permute-start.1
  29.7 1.0 collective-permute-start.2
  30.7 5.1 %collective-permute-done = bf16[8,2,32,256]{3,2,0,1:T(8,128)(2,1)S(1)} collective-permute-done((bf16[8,2,32,256]{3,2,0,1:T(8,128)(2,1)S(1)}, bf16[8,2,32,256]{3,2,0,1:T(8,128)(2,1)S(1)}, u32[]{:S(2)}, u32[]{:S(2)}) %collective-permute-start) | collective-permute-done | bytes 262176 | tf_op jit(solution)/shard_map/ppermute | solution.py:38
  35.8 1.3 collective-permute-done.1
  37.1 2.7 %collective-permute-done.2 = bf16[8,2,32,256]{3,2,0,1:T(8,128)(2,1)S(1)} collective-permute-done((bf16[8,2,32,256]{3,2,0,1:T(8,128)(2,1)S(1)}, bf16[8,2,32,256]{3,2,0,1:T(8,128)(2,1)S(1)}, u32[]{:S(2)}, u32[]{:S(2)}) %collective-permute-start.2) | collective-permute-done | bytes 262176 | tf_op jit(solution)/shard_map/ppermute | solution.py:38
  39.8 0.1 pad_maximum_fusion.w0
  39.9 2.8 %collective-permute-start.3 = (bf16[4,8,32,256]{3,2,1,0:T(8,128)(2,1)S(1)}, bf16[4,8,32,256]{3,2,1,0:T(8,128)(2,1)S(1)}, u32[]{:S(2)}, u32[]{:S(2)}) collective-permute-start(bf16[4,8,32,256]{3,2,1,0:T(8,128)(2,1)S(1)} %pad_maximum_fusion.w0), channel_id=1, source_target_pairs={{0,12},{1,13},{2,14},{3,15},{4,0},{5,1},{6,2},{7,3},{8,4},{9,5},{1... | collective-permute-start | bytes 1572872 | tf_op jit(solution)/shard_map/ppermute | solution.py:38
  42.7 0.8 collective-permute-start.4
  43.5 0.9 collective-permute-start.5
  44.4 0.1 pad_maximum_fusion.1.w0
  44.5 2.4 %collective-permute-start.13 = (bf16[4,8,32,256]{3,2,1,0:T(8,128)(2,1)S(1)}, bf16[4,8,32,256]{3,2,1,0:T(8,128)(2,1)S(1)}, u32[]{:S(2)}, u32[]{:S(2)}) collective-permute-start(bf16[4,8,32,256]{3,2,1,0:T(8,128)(2,1)S(1)} %pad_maximum_fusion.1.w0), channel_id=1, source_target_pairs={{0,12},{1,13},{2,14},{3,15},{4,0},{5,1},{6,2},{7,3},{8,4},{9,5},{1... | collective-permute-start | bytes 1572872 | tf_op jit(solution)/shard_map/ppermute | solution.py:38
  46.9 8.2 %collective-permute-done.3.w1 = bf16[4,8,32,256]{3,2,1,0:T(8,128)(2,1)S(1)} collective-permute-done((bf16[4,8,32,256]{3,2,1,0:T(8,128)(2,1)S(1)}, bf16[4,8,32,256]{3,2,1,0:T(8,128)(2,1)S(1)}, u32[]{:S(2)}, u32[]{:S(2)}) %collective-permute-start.3) | collective-permute-done | bytes 524320 | tf_op jit(solution)/shard_map/ppermute | solution.py:38
  55.1 4.5 %collective-permute-start.15 = (bf16[4,8,32,256]{3,2,1,0:T(8,128)(2,1)S(1)}, bf16[4,8,32,256]{3,2,1,0:T(8,128)(2,1)S(1)}, u32[]{:S(2)}, u32[]{:S(2)}) collective-permute-start(bf16[4,8,32,256]{3,2,1,0:T(8,128)(2,1)S(1)} %pad_maximum_fusion.1.w0), channel_id=1, source_target_pairs={{0,4},{1,5},{2,6},{3,7},{4,8},{5,9},{6,10},{7,11},{8,12},{9,13},{1... | collective-permute-start | bytes 1572872 | tf_op jit(solution)/shard_map/ppermute | solution.py:38
  59.6 9.7 %head.2 = (bf16[4,8,32,256]{3,2,1,0:T(8,128)(2,1)S(1)}, bf16[4,8,32,256]{3,2,1,0:T(8,128)(2,1)S(1)}, bf16[4,8,32,256]{3,2,1,0:T(8,128)(2,1)S(1)}, bf16[4,8,32,256]{3,2,1,0:T(8,128)(2,1)S(1)}) custom-call(s32[1]{0:T(128)} %constant.26.clone.1.which, s32[8]{0:T(128)S(1)} %stack.42.where, bf16[4,8,32,256]{3,2,1,0:T(8,128)(2,1)S(1)} %pad_maximum_fusion.w0, ...), custom_call_target="tpu_custom_call" | custom-call | flops 8000000000 | bytes 16000000 | tf_op jit(solution)/shard_map/head/pallas_call | solution.py:306
  69.3 0.7 collective-permute-start.7
  70.0 0.3 collective-permute-start.8
  70.2 3.0 %collective-permute-start.9 = (bf16[4,8,32,256]{3,2,1,0:T(8,128)(2,1)S(1)}, bf16[4,8,32,256]{3,2,1,0:T(8,128)(2,1)S(1)}, u32[]{:S(2)}, u32[]{:S(2)}) collective-permute-start(bf16[4,8,32,256]{3,2,1,0:T(8,128)(2,1)S(1)} %get-tuple-element.17), channel_id=1, source_target_pairs={{0,12},{1,13},{2,14},{3,15},{4,0},{5,1},{6,2},{7,3},{8,4},{9,5},{1... | collective-permute-start | bytes 1572872 | tf_op jit(solution)/shard_map/ppermute | solution.py:38
  73.2 9.6 %head.3 = (bf16[4,8,32,256]{3,2,1,0:T(8,128)(2,1)S(1)}, bf16[4,8,32,256]{3,2,1,0:T(8,128)(2,1)S(1)}, bf16[4,8,32,256]{3,2,1,0:T(8,128)(2,1)S(1)}, bf16[4,8,32,256]{3,2,1,0:T(8,128)(2,1)S(1)}) custom-call(s32[1]{0:T(128)} %constant.27.clone.1.which, s32[8]{0:T(128)S(1)} %stack.42.where, bf16[4,8,32,256]{3,2,1,0:T(8,128)(2,1)S(1)} %pad_maximum_fusion.1.w0, ...), custom_call_target="tpu_custom_call" | custom-call | flops 8000000000 | bytes 16000000 | tf_op jit(solution)/shard_map/head/pallas_call | solution.py:306
  82.8 1.8 %collective-permute-start.16 = (bf16[4,8,32,256]{3,2,1,0:T(8,128)(2,1)S(1)}, bf16[4,8,32,256]{3,2,1,0:T(8,128)(2,1)S(1)}, u32[]{:S(2)}, u32[]{:S(2)}) collective-permute-start(bf16[4,8,32,256]{3,2,1,0:T(8,128)(2,1)S(1)} %get-tuple-element.19), channel_id=1, source_target_pairs={{0,8},{1,9},{2,10},{3,11},{4,12},{5,13},{6,14},{7,15},{8,0},{9,1},... | collective-permute-start | bytes 1572872 | tf_op jit(solution)/shard_map/ppermute | solution.py:38
  84.6 0.0 collective-permute-start.17
  84.7 3.2 %collective-permute-start.18 = (bf16[4,8,32,256]{3,2,1,0:T(8,128)(2,1)S(1)}, bf16[4,8,32,256]{3,2,1,0:T(8,128)(2,1)S(1)}, u32[]{:S(2)}, u32[]{:S(2)}) collective-permute-start(bf16[4,8,32,256]{3,2,1,0:T(8,128)(2,1)S(1)} %get-tuple-element.21), channel_id=1, source_target_pairs={{0,12},{1,13},{2,14},{3,15},{4,0},{5,1},{6,2},{7,3},{8,4},{9,5},{1... | collective-permute-start | bytes 1572872 | tf_op jit(solution)/shard_map/ppermute | solution.py:38
  87.9 0.4 add_convert_fusion.1
  88.3 0.1 collective-permute-start.10
  88.4 2.1 %collective-permute-start.11 = (bf16[8,32,256]{2,1,0:T(8,128)(2,1)S(1)}, bf16[8,32,256]{2,1,0:T(8,128)(2,1)S(1)}, u32[]{:S(2)}, u32[]{:S(2)}) collective-permute-start(bf16[8,32,256]{2,1,0:T(8,128)(2,1)S(1)} %get-tuple-element.24), channel_id=1, source_target_pairs={{0,2},{1,3},{2,0},{3,1},{4,6},{5,7},{6,4},{7,5},{8,10},{9,11},{10,... | collective-permute-start | bytes 393224 | tf_op jit(solution)/shard_map/ppermute | solution.py:38
  90.5 3.8 %collective-permute-done.16 = bf16[4,8,32,256]{3,2,1,0:T(8,128)(2,1)S(1)} collective-permute-done((bf16[4,8,32,256]{3,2,1,0:T(8,128)(2,1)S(1)}, bf16[4,8,32,256]{3,2,1,0:T(8,128)(2,1)S(1)}, u32[]{:S(2)}, u32[]{:S(2)}) %collective-permute-start.16) | collective-permute-done | bytes 524320 | tf_op jit(solution)/shard_map/ppermute | solution.py:38
  94.2 0.6 collective-permute-start.12
  94.8 7.7 %collective-permute-done.17 = bf16[4,8,32,256]{3,2,1,0:T(8,128)(2,1)S(1)} collective-permute-done((bf16[4,8,32,256]{3,2,1,0:T(8,128)(2,1)S(1)}, bf16[4,8,32,256]{3,2,1,0:T(8,128)(2,1)S(1)}, u32[]{:S(2)}, u32[]{:S(2)}) %collective-permute-start.17) | collective-permute-done | bytes 524320 | tf_op jit(solution)/shard_map/ppermute | solution.py:38
  102.6 0.1 collective-permute-done.18
  102.6 0.4 add_convert_fusion
  103.1 0.1 collective-permute-start.19
  103.1 1.2 collective-permute-start.20
  104.4 2.0 %collective-permute-start.21 = (bf16[8,32,256]{2,1,0:T(8,128)(2,1)S(1)}, bf16[8,32,256]{2,1,0:T(8,128)(2,1)S(1)}, u32[]{:S(2)}, u32[]{:S(2)}) collective-permute-start(bf16[8,32,256]{2,1,0:T(8,128)(2,1)S(1)} %get-tuple-element.26), channel_id=1, source_target_pairs={{0,3},{1,0},{2,1},{3,2},{4,7},{5,4},{6,5},{7,6},{8,11},{9,8},{10,9... | collective-permute-start | bytes 393224 | tf_op jit(solution)/shard_map/ppermute | solution.py:38
  106.4 0.1 fusion.6
  106.5 4.3 %collective-permute-done.19 = bf16[8,32,256]{2,1,0:T(8,128)(2,1)S(1)} collective-permute-done((bf16[8,32,256]{2,1,0:T(8,128)(2,1)S(1)}, bf16[8,32,256]{2,1,0:T(8,128)(2,1)S(1)}, u32[]{:S(2)}, u32[]{:S(2)}) %collective-permute-start.19) | collective-permute-done | bytes 131104 | tf_op jit(solution)/shard_map/ppermute | solution.py:38
  110.7 0.9 collective-permute-done.21
  111.6 0.1 fusion.7
  111.7 13.1 %all_to_all.16.parts = bf16[8,2,32,256]{3,2,1,0:T(8,128)(2,1)S(1)} all-to-all(bf16[8,2,32,256]{3,2,1,0:T(8,128)(2,1)S(1)} %pad_maximum_fusion.2), channel_id=1, replica_groups=mesh['r'=2,'z'=8,'x'=4,'y'=4] {'z'}, dimensions={0} | all-to-all | bytes 524288 | tf_op jit(solution)/shard_map/all_to_all | solution.py:46
  124.8 0.1 collective-permute-start.22
  124.9 1.2 collective-permute-done.22.theirs
  126.2 0.2 squares.1
  126.4 19.3 %all_to_all.17.squares = f32[128,1,128]{2,1,0:T(1,128)S(1)} all-to-all(f32[128,1,128]{2,1,0:T(1,128)S(1)} %squares.1), channel_id=1, replica_groups=mesh['r'=2,'z'=8,'x'=4,'y'=4] {'z','x','y'}, dimensions={0} | all-to-all | bytes 131072 | tf_op jit(solution)/shard_map/all_to_all | solution.py:46
  145.6 1.5 %finish.1 = (f32[32,512]{1,0:T(8,128)}, f32[32,512]{1,0:T(8,128)}) custom-call(s32[8]{0:T(128)S(1)} %stack.42.where, f32[128,1,128]{2,1,0:T(1,128)S(1)} %all_to_all.17.squares, f32[2,32,256]{2,1,0:T(8,128)S(1)} %gather_sum.1.full, f32[2,32,256]{2,1,0:T(8,128)S(1)} %collective-permute-done.22.theirs), custom_call_target="tpu_custom_call" | custom-call | tf_op jit(solution)/shard_map/finish/pallas_call | solution.py:201
  (26 shorter events, 0.3 us)
Async XLA Ops:
  5.6 54.0 %copy-start = (bf16[512,2048]{1,0:T(8,128)(2,1)S(1)}, bf16[512,2048]{1,0:T(8,128)(2,1)}, u32[]{:S(2)}) copy-start(bf16[512,2048]{1,0:T(8,128)(2,1)} %queries.5) | copy-start | bytes 6291460
  5.6 54.0 %collective-permute-start.6 = (bf16[512,6144]{1,0:T(8,128)(2,1)S(1)}, bf16[512,6144]{1,0:T(8,128)(2,1)S(1)}, u32[]{:S(2)}, u32[]{:S(2)}) collective-permute-start(bf16[512,6144]{1,0:T(8,128)(2,1)S(1)} %get-tuple-element.12.sent), channel_id=1, source_target_pairs={{0,128},{128,0},{1,129},{129,1},{2,130},{130,2},{3,131},{131,3},{4... | collective-permute-start | bytes 18874376 | tf_op jit(solution)/shard_map/ppermute | solution.py:42
  26.0 9.8 %collective-permute-start = (bf16[8,2,32,256]{3,2,0,1:T(8,128)(2,1)S(1)}, bf16[8,2,32,256]{3,2,0,1:T(8,128)(2,1)S(1)}, u32[]{:S(2)}, u32[]{:S(2)}) collective-permute-start(bf16[8,2,32,256]{3,2,0,1:T(8,128)(2,1)S(1)} %copy.9), channel_id=1, source_target_pairs={{0,3},{1,0},{2,1},{3,2},{4,7},{5,4},{6,5},{7,6},{8,11},{9,8},{10,9... | collective-permute-start | bytes 786440 | tf_op jit(solution)/shard_map/ppermute | solution.py:38
  29.1 8.0 %collective-permute-start.1 = (bf16[8,2,32,256]{3,2,0,1:T(8,128)(2,1)S(1)}, bf16[8,2,32,256]{3,2,0,1:T(8,128)(2,1)S(1)}, u32[]{:S(2)}, u32[]{:S(2)}) collective-permute-start(bf16[8,2,32,256]{3,2,0,1:T(8,128)(2,1)S(1)} %copy.9), channel_id=1, source_target_pairs={{0,2},{1,3},{2,0},{3,1},{4,6},{5,7},{6,4},{7,5},{8,10},{9,11},{10,... | collective-permute-start | bytes 786440 | tf_op jit(solution)/shard_map/ppermute | solution.py:38
  29.7 10.1 %collective-permute-start.2 = (bf16[8,2,32,256]{3,2,0,1:T(8,128)(2,1)S(1)}, bf16[8,2,32,256]{3,2,0,1:T(8,128)(2,1)S(1)}, u32[]{:S(2)}, u32[]{:S(2)}) collective-permute-start(bf16[8,2,32,256]{3,2,0,1:T(8,128)(2,1)S(1)} %copy.9), channel_id=1, source_target_pairs={{0,1},{1,2},{2,3},{3,0},{4,5},{5,6},{6,7},{7,4},{8,9},{9,10},{10,1... | collective-permute-start | bytes 786440 | tf_op jit(solution)/shard_map/ppermute | solution.py:38
  39.9 15.2 %collective-permute-start.3 = (bf16[4,8,32,256]{3,2,1,0:T(8,128)(2,1)S(1)}, bf16[4,8,32,256]{3,2,1,0:T(8,128)(2,1)S(1)}, u32[]{:S(2)}, u32[]{:S(2)}) collective-permute-start(bf16[4,8,32,256]{3,2,1,0:T(8,128)(2,1)S(1)} %pad_maximum_fusion.w0), channel_id=1, source_target_pairs={{0,12},{1,13},{2,14},{3,15},{4,0},{5,1},{6,2},{7,3},{8,4},{9,5},{1... | collective-permute-start | bytes 1572872 | tf_op jit(solution)/shard_map/ppermute | solution.py:38
  42.7 12.4 %collective-permute-start.4 = (bf16[4,8,32,256]{3,2,1,0:T(8,128)(2,1)S(1)}, bf16[4,8,32,256]{3,2,1,0:T(8,128)(2,1)S(1)}, u32[]{:S(2)}, u32[]{:S(2)}) collective-permute-start(bf16[4,8,32,256]{3,2,1,0:T(8,128)(2,1)S(1)} %pad_maximum_fusion.w0), channel_id=1, source_target_pairs={{0,8},{1,9},{2,10},{3,11},{4,12},{5,13},{6,14},{7,15},{8,0},{9,1},... | collective-permute-start | bytes 1572872 | tf_op jit(solution)/shard_map/ppermute | solution.py:38
  43.5 16.1 %collective-permute-start.5 = (bf16[4,8,32,256]{3,2,1,0:T(8,128)(2,1)S(1)}, bf16[4,8,32,256]{3,2,1,0:T(8,128)(2,1)S(1)}, u32[]{:S(2)}, u32[]{:S(2)}) collective-permute-start(bf16[4,8,32,256]{3,2,1,0:T(8,128)(2,1)S(1)} %pad_maximum_fusion.w0), channel_id=1, source_target_pairs={{0,4},{1,5},{2,6},{3,7},{4,8},{5,9},{6,10},{7,11},{8,12},{9,13},{1... | collective-permute-start | bytes 1572872 | tf_op jit(solution)/shard_map/ppermute | solution.py:38
  44.5 25.8 %collective-permute-start.13 = (bf16[4,8,32,256]{3,2,1,0:T(8,128)(2,1)S(1)}, bf16[4,8,32,256]{3,2,1,0:T(8,128)(2,1)S(1)}, u32[]{:S(2)}, u32[]{:S(2)}) collective-permute-start(bf16[4,8,32,256]{3,2,1,0:T(8,128)(2,1)S(1)} %pad_maximum_fusion.1.w0), channel_id=1, source_target_pairs={{0,12},{1,13},{2,14},{3,15},{4,0},{5,1},{6,2},{7,3},{8,4},{9,5},{1... | collective-permute-start | bytes 1572872 | tf_op jit(solution)/shard_map/ppermute | solution.py:38
  55.1 18.1 %collective-permute-start.14 = (bf16[4,8,32,256]{3,2,1,0:T(8,128)(2,1)S(1)}, bf16[4,8,32,256]{3,2,1,0:T(8,128)(2,1)S(1)}, u32[]{:S(2)}, u32[]{:S(2)}) collective-permute-start(bf16[4,8,32,256]{3,2,1,0:T(8,128)(2,1)S(1)} %pad_maximum_fusion.1.w0), channel_id=1, source_target_pairs={{0,8},{1,9},{2,10},{3,11},{4,12},{5,13},{6,14},{7,15},{8,0},{9,1},... | collective-permute-start | bytes 1572872 | tf_op jit(solution)/shard_map/ppermute | solution.py:38
  55.1 18.1 %collective-permute-start.15 = (bf16[4,8,32,256]{3,2,1,0:T(8,128)(2,1)S(1)}, bf16[4,8,32,256]{3,2,1,0:T(8,128)(2,1)S(1)}, u32[]{:S(2)}, u32[]{:S(2)}) collective-permute-start(bf16[4,8,32,256]{3,2,1,0:T(8,128)(2,1)S(1)} %pad_maximum_fusion.1.w0), channel_id=1, source_target_pairs={{0,4},{1,5},{2,6},{3,7},{4,8},{5,9},{6,10},{7,11},{8,12},{9,13},{1... | collective-permute-start | bytes 1572872 | tf_op jit(solution)/shard_map/ppermute | solution.py:38
  69.3 15.4 %collective-permute-start.7 = (bf16[4,8,32,256]{3,2,1,0:T(8,128)(2,1)S(1)}, bf16[4,8,32,256]{3,2,1,0:T(8,128)(2,1)S(1)}, u32[]{:S(2)}, u32[]{:S(2)}) collective-permute-start(bf16[4,8,32,256]{3,2,1,0:T(8,128)(2,1)S(1)} %get-tuple-element.15), channel_id=1, source_target_pairs={{0,8},{1,9},{2,10},{3,11},{4,12},{5,13},{6,14},{7,15},{8,0},{9,1},... | collective-permute-start | bytes 1572872 | tf_op jit(solution)/shard_map/ppermute | solution.py:38
  70.0 17.9 %collective-permute-start.8 = (bf16[4,8,32,256]{3,2,1,0:T(8,128)(2,1)S(1)}, bf16[4,8,32,256]{3,2,1,0:T(8,128)(2,1)S(1)}, u32[]{:S(2)}, u32[]{:S(2)}) collective-permute-start(bf16[4,8,32,256]{3,2,1,0:T(8,128)(2,1)S(1)} %get-tuple-element.16), channel_id=1, source_target_pairs={{0,4},{1,5},{2,6},{3,7},{4,8},{5,9},{6,10},{7,11},{8,12},{9,13},{1... | collective-permute-start | bytes 1572872 | tf_op jit(solution)/shard_map/ppermute | solution.py:38
  70.2 17.7 %collective-permute-start.9 = (bf16[4,8,32,256]{3,2,1,0:T(8,128)(2,1)S(1)}, bf16[4,8,32,256]{3,2,1,0:T(8,128)(2,1)S(1)}, u32[]{:S(2)}, u32[]{:S(2)}) collective-permute-start(bf16[4,8,32,256]{3,2,1,0:T(8,128)(2,1)S(1)} %get-tuple-element.17), channel_id=1, source_target_pairs={{0,12},{1,13},{2,14},{3,15},{4,0},{5,1},{6,2},{7,3},{8,4},{9,5},{1... | collective-permute-start | bytes 1572872 | tf_op jit(solution)/shard_map/ppermute | solution.py:38
  82.8 11.4 %collective-permute-start.16 = (bf16[4,8,32,256]{3,2,1,0:T(8,128)(2,1)S(1)}, bf16[4,8,32,256]{3,2,1,0:T(8,128)(2,1)S(1)}, u32[]{:S(2)}, u32[]{:S(2)}) collective-permute-start(bf16[4,8,32,256]{3,2,1,0:T(8,128)(2,1)S(1)} %get-tuple-element.19), channel_id=1, source_target_pairs={{0,8},{1,9},{2,10},{3,11},{4,12},{5,13},{6,14},{7,15},{8,0},{9,1},... | collective-permute-start | bytes 1572872 | tf_op jit(solution)/shard_map/ppermute | solution.py:38
  84.6 17.9 %collective-permute-start.17 = (bf16[4,8,32,256]{3,2,1,0:T(8,128)(2,1)S(1)}, bf16[4,8,32,256]{3,2,1,0:T(8,128)(2,1)S(1)}, u32[]{:S(2)}, u32[]{:S(2)}) collective-permute-start(bf16[4,8,32,256]{3,2,1,0:T(8,128)(2,1)S(1)} %get-tuple-element.20), channel_id=1, source_target_pairs={{0,4},{1,5},{2,6},{3,7},{4,8},{5,9},{6,10},{7,11},{8,12},{9,13},{1... | collective-permute-start | bytes 1572872 | tf_op jit(solution)/shard_map/ppermute | solution.py:38
  84.7 18.0 %collective-permute-start.18 = (bf16[4,8,32,256]{3,2,1,0:T(8,128)(2,1)S(1)}, bf16[4,8,32,256]{3,2,1,0:T(8,128)(2,1)S(1)}, u32[]{:S(2)}, u32[]{:S(2)}) collective-permute-start(bf16[4,8,32,256]{3,2,1,0:T(8,128)(2,1)S(1)} %get-tuple-element.21), channel_id=1, source_target_pairs={{0,12},{1,13},{2,14},{3,15},{4,0},{5,1},{6,2},{7,3},{8,4},{9,5},{1... | collective-permute-start | bytes 1572872 | tf_op jit(solution)/shard_map/ppermute | solution.py:38
  88.3 16.0 %collective-permute-start.10 = (bf16[8,32,256]{2,1,0:T(8,128)(2,1)S(1)}, bf16[8,32,256]{2,1,0:T(8,128)(2,1)S(1)}, u32[]{:S(2)}, u32[]{:S(2)}) collective-permute-start(bf16[8,32,256]{2,1,0:T(8,128)(2,1)S(1)} %get-tuple-element.22), channel_id=1, source_target_pairs={{0,1},{1,2},{2,3},{3,0},{4,5},{5,6},{6,7},{7,4},{8,9},{9,10},{10,1... | collective-permute-start | bytes 393224 | tf_op jit(solution)/shard_map/ppermute | solution.py:38
  88.4 18.0 %collective-permute-start.11 = (bf16[8,32,256]{2,1,0:T(8,128)(2,1)S(1)}, bf16[8,32,256]{2,1,0:T(8,128)(2,1)S(1)}, u32[]{:S(2)}, u32[]{:S(2)}) collective-permute-start(bf16[8,32,256]{2,1,0:T(8,128)(2,1)S(1)} %get-tuple-element.24), channel_id=1, source_target_pairs={{0,2},{1,3},{2,0},{3,1},{4,6},{5,7},{6,4},{7,5},{8,10},{9,11},{10,... | collective-permute-start | bytes 393224 | tf_op jit(solution)/shard_map/ppermute | solution.py:38
  94.2 12.2 %collective-permute-start.12 = (bf16[8,32,256]{2,1,0:T(8,128)(2,1)S(1)}, bf16[8,32,256]{2,1,0:T(8,128)(2,1)S(1)}, u32[]{:S(2)}, u32[]{:S(2)}) collective-permute-start(bf16[8,32,256]{2,1,0:T(8,128)(2,1)S(1)} %get-tuple-element.23), channel_id=1, source_target_pairs={{0,3},{1,0},{2,1},{3,2},{4,7},{5,4},{6,5},{7,6},{8,11},{9,8},{10,9... | collective-permute-start | bytes 393224 | tf_op jit(solution)/shard_map/ppermute | solution.py:38
  103.1 7.7 %collective-permute-start.19 = (bf16[8,32,256]{2,1,0:T(8,128)(2,1)S(1)}, bf16[8,32,256]{2,1,0:T(8,128)(2,1)S(1)}, u32[]{:S(2)}, u32[]{:S(2)}) collective-permute-start(bf16[8,32,256]{2,1,0:T(8,128)(2,1)S(1)} %get-tuple-element.25), channel_id=1, source_target_pairs={{0,1},{1,2},{2,3},{3,0},{4,5},{5,6},{6,7},{7,4},{8,9},{9,10},{10,1... | collective-permute-start | bytes 393224 | tf_op jit(solution)/shard_map/ppermute | solution.py:38
  103.1 7.6 %collective-permute-start.20 = (bf16[8,32,256]{2,1,0:T(8,128)(2,1)S(1)}, bf16[8,32,256]{2,1,0:T(8,128)(2,1)S(1)}, u32[]{:S(2)}, u32[]{:S(2)}) collective-permute-start(bf16[8,32,256]{2,1,0:T(8,128)(2,1)S(1)} %get-tuple-element.27), channel_id=1, source_target_pairs={{0,2},{1,3},{2,0},{3,1},{4,6},{5,7},{6,4},{7,5},{8,10},{9,11},{10,... | collective-permute-start | bytes 393224 | tf_op jit(solution)/shard_map/ppermute | solution.py:38
  104.4 7.3 %collective-permute-start.21 = (bf16[8,32,256]{2,1,0:T(8,128)(2,1)S(1)}, bf16[8,32,256]{2,1,0:T(8,128)(2,1)S(1)}, u32[]{:S(2)}, u32[]{:S(2)}) collective-permute-start(bf16[8,32,256]{2,1,0:T(8,128)(2,1)S(1)} %get-tuple-element.26), channel_id=1, source_target_pairs={{0,3},{1,0},{2,1},{3,2},{4,7},{5,4},{6,5},{7,6},{8,11},{9,8},{10,9... | collective-permute-start | bytes 393224 | tf_op jit(solution)/shard_map/ppermute | solution.py:38
  124.8 1.3 collective-permute-start.22
